TPU v7x, 32 devices: a whole 2x2x4 slice. The times are simulated.
32 devices in a mesh: dom: 4 (over z), grp: 8 (over y, x, core).
Axes of the slice: x: 2, y: 2, z: 4, core: 2. Of those that a mesh axis runs over, the one named last changes fastest.
Arguments:
- master_rows: bfloat16 [8, 512, 512], P('grp', 'dom'), may hold values from -6 to 6
- cotangent: bfloat16 [8, 512, 512], P('grp', 'dom'), may hold values from -6 to 6
- relation_weight: bfloat16 [4, 512, 512], replicated, may hold values from -0.125 to 0.125
- self_weight: bfloat16 [512, 512], replicated, may hold values from -0.25 to 0.25
- edge_source: int32 [8, 8192], P('grp', 'dom'), may hold values from 0 to 191
- edge_target: int32 [8, 8192], P('grp', 'dom'), may hold values from 0 to 191
- edge_relation: int32 [8, 8192], P('grp', 'dom'), may hold values from 0 to 3
- send_rows: int32 [8, 256], P('grp', 'dom'), may hold values from 0 to 127
- send_counts: int32 [8, 16], P('grp', 'dom'), may hold values from 4 to 16, as said below
Outputs:
- activation: bfloat16 [8, 512, 512], P('grp', 'dom')
- input_grad: bfloat16 [8, 512, 512], P('grp', 'dom')
- weight_grads: float32 [5, 512, 512], P(None, 'grp')
Inputs may be any that keep to these rules, and one draw needn't show every extreme that they name: `send_counts`: on every device the count for some peer is exactly 16.
All inputs are finite; a program needn't handle non-finite values.
Results may differ from a plain program's by a relative error of at most 0.0061.
Values may be sent and summed in bfloat16 or wider, within the bound.
No kernel may reach another device: no remote copies, remote signals or barrier semaphores. Data moves between devices by JAX's collectives and lax.ppermute only.
A program may use at most 64 MiB of HBM per device.

v0:
```python
import jax
import jax.numpy as jnp
from jax import lax
from jax.sharding import PartitionSpec as P


def pull_rows(table, send_rows, valid):
    domains = lax.axis_size("dom")
    width = table.shape[1]
    picked = table[send_rows]
    picked = jnp.where(valid[:, None], picked, jnp.zeros_like(picked))
    moved = lax.all_to_all(
        picked.reshape(domains, -1, width), "dom", split_axis=0, concat_axis=0, tiled=True
    )
    return jnp.concatenate([table, moved.reshape(-1, width)], axis=0)


def push_rows(mirror_part, placement, own):
    domains = lax.axis_size("dom")
    width = own.shape[1]
    moved = lax.all_to_all(
        mirror_part.reshape(domains, -1, width), "dom", split_axis=0, concat_axis=0, tiled=True
    )
    return own + jnp.dot(placement, moved.reshape(-1, width), preferred_element_type=jnp.float32)


def edge_counts(sources, targets, relation, relations, local_rows):
    flat_index = (relation * local_rows + targets) * local_rows + sources
    ones = jnp.ones(sources.shape, jnp.float32)
    counted = jax.ops.segment_sum(
        ones, flat_index, num_segments=relations * local_rows * local_rows
    )
    return counted.reshape(relations, local_rows, local_rows).astype(jnp.bfloat16)


def per_device(
    master_rows,
    cotangent,
    relation_weight,
    self_weight,
    edge_source,
    edge_target,
    edge_relation,
    send_rows,
    send_counts,
):
    masters = master_rows[0]
    cotan = cotangent[0]
    sources = edge_source[0]
    targets = edge_target[0]
    relation = edge_relation[0]
    slots = send_rows[0]
    counts = send_counts[0]
    domains = lax.axis_size("dom")
    relations = relation_weight.shape[0]
    master_count = masters.shape[0]
    capacity = slots.shape[0] // domains
    valid = (jnp.arange(capacity)[None, :] < counts[:, None]).reshape(-1)
    placement = ((slots[None, :] == jnp.arange(master_count)[:, None]) & valid[None, :]).astype(
        jnp.bfloat16
    )
    table = pull_rows(masters, slots, valid)
    local_rows = table.shape[0]
    adjacency = edge_counts(sources, targets, relation, relations, local_rows)
    aggregated = jnp.einsum(
        "rij,jd->rid", adjacency, table, preferred_element_type=jnp.float32
    ).astype(jnp.bfloat16)
    partial_value = jnp.einsum(
        "rnd,rde->ne", aggregated, relation_weight, preferred_element_type=jnp.float32
    )
    own = partial_value[:master_count] + jnp.dot(
        masters, self_weight, preferred_element_type=jnp.float32
    )
    z_value = push_rows(partial_value[master_count:].astype(jnp.bfloat16), placement, own)
    activation = jax.nn.silu(z_value).astype(jnp.bfloat16)
    sigmoid_z = jax.nn.sigmoid(z_value)
    grad_z = (cotan.astype(jnp.float32) * sigmoid_z * (1.0 + z_value * (1.0 - sigmoid_z))).astype(
        jnp.bfloat16
    )
    grad_table = pull_rows(grad_z, slots, valid)
    relation_grad = jnp.einsum(
        "rnd,ne->rde", aggregated, grad_table, preferred_element_type=jnp.float32
    )
    self_grad = jnp.dot(masters.T, grad_z, preferred_element_type=jnp.float32)
    local_grads = jnp.concatenate([relation_grad, self_grad[None]], axis=0)
    group_part = lax.psum_scatter(local_grads, "grp", scatter_dimension=1, tiled=True)
    weight_grads = lax.psum(group_part, "dom")
    back = jnp.einsum(
        "rij,id->rjd", adjacency, grad_table, preferred_element_type=jnp.float32
    ).astype(jnp.bfloat16)
    back_partial = jnp.einsum(
        "rne,rde->nd", back, relation_weight, preferred_element_type=jnp.float32
    )
    back_own = back_partial[:master_count] + jnp.dot(
        grad_z, self_weight.T, preferred_element_type=jnp.float32
    )
    input_grad = push_rows(back_partial[master_count:].astype(jnp.bfloat16), placement, back_own)
    return (activation[None], input_grad.astype(jnp.bfloat16)[None], weight_grads)


def solution(mesh):
    return jax.shard_map(
        per_device,
        mesh=mesh,
        in_specs=(
            P("grp", "dom", None),
            P("grp", "dom", None),
            P(),
            P(),
            P("grp", "dom"),
            P("grp", "dom"),
            P("grp", "dom"),
            P("grp", "dom"),
            P("grp", "dom"),
        ),
        out_specs=(P("grp", "dom", None), P("grp", "dom", None), P(None, "grp", None)),
        check_vma=False,
    )
```

profile of v0, /device:TPU:0, one launch (start us, length us, event | category | flops | bytes accessed | tf_op | source)
XLA Modules:
  0.0 171.5 jit_solution(12031938624284277153)
XLA Ops:
  7.2 0.9 iota_compare_fusion.1
  8.8 1.6 gather_fusion
  11.1 6.3 %all-to-all-start = ((bf16[4,16,512]{2,1,0:T(8,128)(2,1)}), bf16[4,16,512]{2,1,0:T(8,128)(2,1)}, u32[]{:S(2)}, u32[]{:S(2)}) async-start(bf16[4,16,512]{2,1,0:T(8,128)(2,1)} %broadcast_select_fusion.1), calls=%async_computation | async-start | bytes 131072 | tf_op jit(solution)/shard_map/all_to_all | solution.py:12
  17.4 0.7 multiply_add_fusion
  18.2 11.4 %scatter_custom_fusion = f32[147456]{0:T(1024)S(1)} fusion(s32[2048]{0:T(1024)S(1)} %bitcast.64, f32[2048]{0:T(1024)S(1)} %broadcast.65, f32[]{:T(128)} %constant.6.clone.1), kind=kCustom, calls=%fused_computation.16 | custom fusion | flops 2048 | bytes 589828 | tf_op jit(solution)/shard_map/scatter-add | solution.py:30
  29.9 1.2 convolution_convert_fusion.1
  31.8 0.7 copy-done.3
  33.1 5.1 %all-to-all-start.1 = ((bf16[4,16,512]{2,1,0:T(8,128)(2,1)}), bf16[4,16,512]{2,1,0:T(8,128)(2,1)S(1)}, u32[]{:S(2)}, u32[]{:S(2)}) async-start(bf16[4,16,512]{2,1,0:T(8,128)(2,1)} %bitcast.10), calls=%async_computation.1 | async-start | bytes 131072 | tf_op jit(solution)/shard_map/all_to_all | solution.py:21
  38.3 5.7 %all-to-all-done.1 = bf16[4,16,512]{2,1,0:T(8,128)(2,1)S(1)} async-done(((bf16[4,16,512]{2,1,0:T(8,128)(2,1)}), bf16[4,16,512]{2,1,0:T(8,128)(2,1)S(1)}, u32[]{:S(2)}, u32[]{:S(2)}) %all-to-all-start.1) | async-done | bytes 65568 | tf_op jit(solution)/shard_map/all_to_all | solution.py:21
  44.1 2.2 %fusion.9 = (bf16[128,512]{1,0:T(8,128)(2,1)S(1)}, bf16[1,128,512]{2,1,0:T(8,128)(2,1)}) fusion(bf16[1,128,512]{2,1,0:T(8,128)(2,1)} %param.10, f32[128,512]{1,0:T(8,128)S(1)} %fusion.17, bf16[512,512]{1,0:T(8,128)(2,1)} %param.12, bf16[1,128,512]{2,1,0:T(8,128)(2,1)S(1)} %copy-done.1, f32[192,512]{1,0:T(8,128)} %copy-done.3), kind=kOutput, calls=%fused_computation.20 | convolution fusion | flops 68026368 | bytes 1572864 | tf_op jit(solution)/shard_map/dot_general | solution.py:71
  46.3 1.3 gather_fusion.1
  47.6 1.5 broadcast_select_fusion
  49.2 3.9 %all-to-all-start.2 = ((bf16[4,16,512]{2,1,0:T(8,128)(2,1)}), bf16[4,16,512]{2,1,0:T(8,128)(2,1)}, u32[]{:S(2)}, u32[]{:S(2)}) async-start(bf16[4,16,512]{2,1,0:T(8,128)(2,1)} %broadcast_select_fusion), calls=%async_computation.2 | async-start | bytes 131072 | tf_op jit(solution)/shard_map/all_to_all | solution.py:12
  53.1 1.3 convolution_bitcast_fusion
  54.5 4.4 %all-to-all-done.2 = bf16[4,16,512]{2,1,0:T(8,128)(2,1)} async-done(((bf16[4,16,512]{2,1,0:T(8,128)(2,1)}), bf16[4,16,512]{2,1,0:T(8,128)(2,1)}, u32[]{:S(2)}, u32[]{:S(2)}) %all-to-all-start.2) | async-done | bytes 65568 | tf_op jit(solution)/shard_map/all_to_all | solution.py:12
  58.9 1.7 fusion.13
  60.6 2.9 %pad_maximum_fusion = f32[5,512,512]{2,1,0:T(8,128)} fusion(f32[1,512,512]{2,1,0:T(8,128)S(1)} %copy-done.2, f32[4,512,512]{2,1,0:T(8,128)S(1)} %fusion.13), kind=kLoop, calls=%fused_computation.3 | loop fusion | flops 1310720 | bytes 10485760 | tf_op jit(solution)/shard_map/concatenate | solution.py:85
  63.5 55.1 %reduce-scatter.2.cloned.1.call-done = f32[5,64,512]{2,1,0:T(8,128)} async-done(((f32[5,512,512]{2,1,0:T(8,128)}), f32[5,64,512]{2,1,0:T(8,128)}) %reduce-scatter.2.cloned.1.call-update) | async-done | bytes 655376 | tf_op jit(solution)/shard_map/reduce_scatter | solution.py:86
  118.7 2.7 %fusion.1 = f32[192,512]{1,0:T(8,128)} fusion(bf16[4,512,512]{2,1,0:T(8,128)(2,1)S(1)} %copy-done, bf16[4,192,192]{2,1,0:T(8,128)(2,1)S(1)} %convert_element_type.31, bf16[64,512]{1,0:T(8,128)(2,1)} %bitcast.15, bf16[128,512]{1,0:T(8,128)(2,1)S(1)} %get-tuple-element.3), kind=kOutput, calls=%fused_computation.8 | convolution fusion | flops 554434560 | bytes 2981888 | tf_op jit(solution)/shard_map/rne,rde->nd/dot_general | solution.py:91
  121.4 0.9 slice.30
  122.3 11.1 %all_to_all.20 = bf16[4,16,512]{2,1,0:T(8,128)(2,1)S(1)} all-to-all(bf16[4,16,512]{2,1,0:T(8,128)(2,1)S(1)} %bitcast.61), channel_id=1, replica_groups=mesh['dom'=4,'grp'=8] {'dom'}, dimensions={0} | all-to-all | bytes 131072 | tf_op jit(solution)/shard_map/all_to_all | solution.py:21
  133.6 1.9 %fusion.5 = bf16[1,128,512]{2,1,0:T(8,128)(2,1)} fusion(f32[128,512]{1,0:T(8,128)S(1)} %fusion.15, bf16[128,512]{1,0:T(8,128)(2,1)S(1)} %get-tuple-element.3, bf16[512,512]{1,0:T(8,128)(2,1)S(1)} %copy-done.4, f32[192,512]{1,0:T(8,128)} %fusion.1), kind=kOutput, calls=%fused_computation.15 | convolution fusion | flops 67305472 | bytes 1310720 | tf_op jit(solution)/shard_map/dot_general | solution.py:94
  135.5 27.2 %all-reduce.2.cloned.1.call-done = f32[5,64,512]{2,1,0:T(8,128)} async-done(((f32[5,64,512]{2,1,0:T(8,128)}), f32[5,64,512]{2,1,0:T(8,128)}) %all-reduce.2.cloned.1.call-update) | async-done | bytes 655376 | tf_op jit(solution)/shard_map/psum | solution.py:87
  162.7 2.0 %copy.15 = f32[5,64,512]{2,1,0:T(8,128)} copy(f32[5,64,512]{2,1,0:T(8,128)} %all-reduce.2.cloned.1.call-done) | data formatting | bytes 1310720
  (27 shorter events, 3.4 us)
Async XLA Ops:
  7.2 24.0 %copy-start = (bf16[4,512,512]{2,1,0:T(8,128)(2,1)S(1)}, bf16[4,512,512]{2,1,0:T(8,128)(2,1)}, u32[]{:S(2)}) copy-start(bf16[4,512,512]{2,1,0:T(8,128)(2,1)} %param.11) | copy-start | bytes 6291460
  7.2 22.8 %copy-start.1 = (bf16[1,128,512]{2,1,0:T(8,128)(2,1)S(1)}, bf16[1,128,512]{2,1,0:T(8,128)(2,1)}, u32[]{:S(2)}) copy-start(bf16[1,128,512]{2,1,0:T(8,128)(2,1)} %param.9) | copy-start | bytes 393220
  11.1 18.8 %all-to-all-start = ((bf16[4,16,512]{2,1,0:T(8,128)(2,1)}), bf16[4,16,512]{2,1,0:T(8,128)(2,1)}, u32[]{:S(2)}, u32[]{:S(2)}) async-start(bf16[4,16,512]{2,1,0:T(8,128)(2,1)} %broadcast_select_fusion.1), calls=%async_computation | async-start | bytes 131072 | tf_op jit(solution)/shard_map/all_to_all | solution.py:12
  31.2 12.8 %copy-start.5 = (s32[1,64]{1,0:T(1,128)S(1)}, s32[1,64]{1,0:T(1,128)}, u32[]{:S(2)}) copy-start(s32[1,64]{1,0:T(1,128)} %param.16) | copy-start | bytes 772
  31.7 0.7 copy-start.3
  33.1 10.8 %all-to-all-start.1 = ((bf16[4,16,512]{2,1,0:T(8,128)(2,1)}), bf16[4,16,512]{2,1,0:T(8,128)(2,1)S(1)}, u32[]{:S(2)}, u32[]{:S(2)}) async-start(bf16[4,16,512]{2,1,0:T(8,128)(2,1)} %bitcast.10), calls=%async_computation.1 | async-start | bytes 131072 | tf_op jit(solution)/shard_map/all_to_all | solution.py:21
  49.2 9.7 %all-to-all-start.2 = ((bf16[4,16,512]{2,1,0:T(8,128)(2,1)}), bf16[4,16,512]{2,1,0:T(8,128)(2,1)}, u32[]{:S(2)}, u32[]{:S(2)}) async-start(bf16[4,16,512]{2,1,0:T(8,128)(2,1)} %broadcast_select_fusion), calls=%async_computation.2 | async-start | bytes 131072 | tf_op jit(solution)/shard_map/all_to_all | solution.py:12
  53.1 65.5 %reduce-scatter.2.cloned.1.call-start = ((), (), s32[]{:S(2)}) async-start(), calls=%async_computation.5 | async-start | bytes 5898240 | tf_op jit(solution)/shard_map/reduce_scatter | solution.py:86
  58.9 1.7 copy-start.2
  63.5 99.2 %all-reduce.2.cloned.1.call-start = ((), (), s32[]{:S(2)}) async-start(), calls=%async_computation.6 | async-start | bytes 1310720 | tf_op jit(solution)/shard_map/psum | solution.py:87
  118.7 14.9 %copy-start.4 = (bf16[512,512]{1,0:T(8,128)(2,1)S(1)}, bf16[512,512]{1,0:T(8,128)(2,1)}, u32[]{:S(2)}) copy-start(bf16[512,512]{1,0:T(8,128)(2,1)} %param.12) | copy-start | bytes 1572868
Sparse Core Ops, SparseCore 0:
  63.6 54.9 reduce-scatter.1
  121.0 41.6 all-reduce.1
where the time goes:
time: 172 us; the launch traced here: 171 us
  waiting for transfers between devices  92.4 us (54%)
  other arithmetic  18.9 us (11%)
  starting transfers between devices  15.4 us (9%)
  between operations  14.2 us (8%)
  matrix products  11.9 us (7%)
  blocking collectives  11.1 us (6%)
  local copies, waits for them, and re-layouts  7.62 us (4%)
    reduce_scatter x1, waiting for transfers between devices, per_device(): lax.psum_scatter(local_grads, 'grp', scatter_dimension=1, tiled=True)  55.1 us
    psum x1, waiting for transfers between devices, per_device(): weight_grads = lax.psum(group_part, 'dom')  27.2 us
    scatter-add x1, other arithmetic, edge_counts(): jax.ops.segment_sum(ones, flat_index, num_segments=relations * local_rows...  11.4 us
    all_to_all x1, blocking collectives, push_rows(): lax.all_to_all(mirror_part.reshape(domains, -1, width), 'dom', split_axis...  11.1 us
    all_to_all x2, starting transfers between devices, pull_rows(): lax.all_to_all(picked.reshape(domains, -1, width), 'dom', split_axis=0, c...  10.2 us
    all_to_all x1, waiting for transfers between devices, push_rows(): lax.all_to_all(mirror_part.reshape(domains, -1, width), 'dom', split_axis...  5.66 us
    all_to_all x1, starting transfers between devices, push_rows(): lax.all_to_all(mirror_part.reshape(domains, -1, width), 'dom', split_axis...  5.08 us
    all_to_all x2, waiting for transfers between devices, pull_rows(): lax.all_to_all(picked.reshape(domains, -1, width), 'dom', split_axis=0, c...  4.44 us
  transfers between devices with their start and end apart: 5, of which 4 were waited for; matrix products, arithmetic and copies ran while one was open for 11% of the time, Pallas kernels for 0%

commit v1 on v0

--- a/solution.py
+++ b/solution.py
@@ -84,7 +84,7 @@
     self_grad = jnp.dot(masters.T, grad_z, preferred_element_type=jnp.float32)
     local_grads = jnp.concatenate([relation_grad, self_grad[None]], axis=0)
     group_part = lax.psum_scatter(local_grads, "grp", scatter_dimension=1, tiled=True)
-    weight_grads = lax.psum(group_part, "dom")
+    weight_grads = jnp.sum(lax.all_gather(group_part, "dom"), axis=0)
     back = jnp.einsum(
         "rij,id->rjd", adjacency, grad_table, preferred_element_type=jnp.float32
     ).astype(jnp.bfloat16)

time: 172 us -> 186 us (1.081)
  waiting for transfers between devices: 92.4 us -> 106 us
  other arithmetic: 18.9 us -> 21.8 us
  local copies, waits for them, and re-layouts: 7.62 us -> 5.64 us
    all_gather x0 -> x1, waiting for transfers between devices: none -> 40.7 us  [per_device(): weight_grads = jnp.sum(lax.all_gather(group_part, 'dom'), axis=0)]
    psum x1 -> x0, waiting for transfers between devices: 27.2 us -> none  [per_device(): weight_grads = lax.psum(group_part, 'dom')]
    reduce_sum x0 -> x1, other arithmetic: none -> 2.93 us  [per_device(): weight_grads = jnp.sum(lax.all_gather(group_part, 'dom'), axis=0)]
    unnamed x13 -> x12, local copies, waits for them, and re-layouts: 2.76 us -> 0.77 us
where the time goes in v1:
time: 186 us; the launch traced here: 185 us
  waiting for transfers between devices  106 us (57%)
  other arithmetic  21.8 us (12%)
  starting transfers between devices  15.4 us (8%)
  between operations  14.2 us (8%)
  matrix products  11.8 us (6%)
  blocking collectives  10.2 us (5%)
  local copies, waits for them, and re-layouts  5.64 us (3%)
    reduce_scatter x1, waiting for transfers between devices, per_device(): lax.psum_scatter(local_grads, 'grp', scatter_dimension=1, tiled=True)  55.1 us
    all_gather x1, waiting for transfers between devices, per_device(): weight_grads = jnp.sum(lax.all_gather(group_part, 'dom'), axis=0)  40.7 us
    scatter-add x1, other arithmetic, edge_counts(): jax.ops.segment_sum(ones, flat_index, num_segments=relations * local_rows...  11.4 us
    all_to_all x2, starting transfers between devices, pull_rows(): lax.all_to_all(picked.reshape(domains, -1, width), 'dom', split_axis=0, c...  10.2 us
    all_to_all x1, blocking collectives, push_rows(): lax.all_to_all(mirror_part.reshape(domains, -1, width), 'dom', split_axis...  10.2 us
    all_to_all x1, waiting for transfers between devices, push_rows(): lax.all_to_all(mirror_part.reshape(domains, -1, width), 'dom', split_axis...  5.66 us
    all_to_all x1, starting transfers between devices, push_rows(): lax.all_to_all(mirror_part.reshape(domains, -1, width), 'dom', split_axis...  5.09 us
    all_to_all x2, waiting for transfers between devices, pull_rows(): lax.all_to_all(picked.reshape(domains, -1, width), 'dom', split_axis=0, c...  4.44 us
  transfers between devices with their start and end apart: 5, of which 4 were waited for; matrix products, arithmetic and copies ran while one was open for 11% of the time, Pallas kernels for 0%

profile of v1, /device:TPU:0, one launch (start us, length us, event | category | flops | bytes accessed | tf_op | source)
XLA Modules:
  0.0 185.1 jit_solution(16081815441345546200)
XLA Ops:
  7.2 0.9 iota_compare_fusion.1
  8.8 1.6 gather_fusion
  11.1 6.3 %all-to-all-start = ((bf16[4,16,512]{2,1,0:T(8,128)(2,1)}), bf16[4,16,512]{2,1,0:T(8,128)(2,1)}, u32[]{:S(2)}, u32[]{:S(2)}) async-start(bf16[4,16,512]{2,1,0:T(8,128)(2,1)} %broadcast_select_fusion.1), calls=%async_computation | async-start | bytes 131072 | tf_op jit(solution)/shard_map/all_to_all | solution.py:12
  17.4 0.7 multiply_add_fusion
  18.2 11.4 %scatter_custom_fusion = f32[147456]{0:T(1024)S(1)} fusion(s32[2048]{0:T(1024)S(1)} %bitcast.66, f32[2048]{0:T(1024)S(1)} %broadcast.65, f32[]{:T(128)} %constant.6.clone.1), kind=kCustom, calls=%fused_computation.16 | custom fusion | flops 2048 | bytes 589828 | tf_op jit(solution)/shard_map/scatter-add | solution.py:30
  29.9 1.2 convolution_convert_fusion.1
  31.7 0.7 copy-done.3
  33.1 5.1 %all-to-all-start.1 = ((bf16[4,16,512]{2,1,0:T(8,128)(2,1)}), bf16[4,16,512]{2,1,0:T(8,128)(2,1)S(1)}, u32[]{:S(2)}, u32[]{:S(2)}) async-start(bf16[4,16,512]{2,1,0:T(8,128)(2,1)} %bitcast.10), calls=%async_computation.1 | async-start | bytes 131072 | tf_op jit(solution)/shard_map/all_to_all | solution.py:21
  38.3 5.7 %all-to-all-done.1 = bf16[4,16,512]{2,1,0:T(8,128)(2,1)S(1)} async-done(((bf16[4,16,512]{2,1,0:T(8,128)(2,1)}), bf16[4,16,512]{2,1,0:T(8,128)(2,1)S(1)}, u32[]{:S(2)}, u32[]{:S(2)}) %all-to-all-start.1) | async-done | bytes 65568 | tf_op jit(solution)/shard_map/all_to_all | solution.py:21
  44.1 2.2 %fusion.9 = (bf16[128,512]{1,0:T(8,128)(2,1)S(1)}, bf16[1,128,512]{2,1,0:T(8,128)(2,1)}) fusion(bf16[1,128,512]{2,1,0:T(8,128)(2,1)} %param.10, f32[128,512]{1,0:T(8,128)S(1)} %fusion.17, bf16[512,512]{1,0:T(8,128)(2,1)} %param.12, bf16[1,128,512]{2,1,0:T(8,128)(2,1)S(1)} %copy-done.1, f32[192,512]{1,0:T(8,128)} %copy-done.3), kind=kOutput, calls=%fused_computation.20 | convolution fusion | flops 68026368 | bytes 1572864 | tf_op jit(solution)/shard_map/dot_general | solution.py:71
  46.3 1.3 gather_fusion.1
  47.6 1.5 broadcast_select_fusion
  49.2 3.9 %all-to-all-start.2 = ((bf16[4,16,512]{2,1,0:T(8,128)(2,1)}), bf16[4,16,512]{2,1,0:T(8,128)(2,1)}, u32[]{:S(2)}, u32[]{:S(2)}) async-start(bf16[4,16,512]{2,1,0:T(8,128)(2,1)} %broadcast_select_fusion), calls=%async_computation.2 | async-start | bytes 131072 | tf_op jit(solution)/shard_map/all_to_all | solution.py:12
  53.1 1.3 convolution_bitcast_fusion
  54.5 4.4 %all-to-all-done.2 = bf16[4,16,512]{2,1,0:T(8,128)(2,1)} async-done(((bf16[4,16,512]{2,1,0:T(8,128)(2,1)}), bf16[4,16,512]{2,1,0:T(8,128)(2,1)}, u32[]{:S(2)}, u32[]{:S(2)}) %all-to-all-start.2) | async-done | bytes 65568 | tf_op jit(solution)/shard_map/all_to_all | solution.py:12
  58.9 1.7 fusion.13
  60.6 2.9 %pad_maximum_fusion = f32[5,512,512]{2,1,0:T(8,128)} fusion(f32[1,512,512]{2,1,0:T(8,128)S(1)} %copy-done.2, f32[4,512,512]{2,1,0:T(8,128)S(1)} %fusion.13), kind=kLoop, calls=%fused_computation.3 | loop fusion | flops 1310720 | bytes 10485760 | tf_op jit(solution)/shard_map/concatenate | solution.py:85
  63.5 55.1 %reduce-scatter.2.cloned.1.call-done = f32[5,64,512]{2,1,0:T(8,128)} async-done(((f32[5,512,512]{2,1,0:T(8,128)}), f32[5,64,512]{2,1,0:T(8,128)}) %reduce-scatter.2.cloned.1.call-update) | async-done | bytes 655376 | tf_op jit(solution)/shard_map/reduce_scatter | solution.py:86
  118.7 2.7 %fusion.1 = f32[192,512]{1,0:T(8,128)} fusion(bf16[4,512,512]{2,1,0:T(8,128)(2,1)S(1)} %copy-done, bf16[4,192,192]{2,1,0:T(8,128)(2,1)S(1)} %convert_element_type.31, bf16[64,512]{1,0:T(8,128)(2,1)} %bitcast.15, bf16[128,512]{1,0:T(8,128)(2,1)S(1)} %get-tuple-element.3), kind=kOutput, calls=%fused_computation.8 | convolution fusion | flops 554434560 | bytes 2981888 | tf_op jit(solution)/shard_map/rne,rde->nd/dot_general | solution.py:91
  121.4 0.9 slice.30
  122.3 10.2 %all_to_all.20 = bf16[4,16,512]{2,1,0:T(8,128)(2,1)S(1)} all-to-all(bf16[4,16,512]{2,1,0:T(8,128)(2,1)S(1)} %bitcast.63), channel_id=1, replica_groups=mesh['dom'=4,'grp'=8] {'dom'}, dimensions={0} | all-to-all | bytes 131072 | tf_op jit(solution)/shard_map/all_to_all | solution.py:21
  132.7 1.9 %fusion.5 = bf16[1,128,512]{2,1,0:T(8,128)(2,1)} fusion(f32[128,512]{1,0:T(8,128)S(1)} %fusion.15, bf16[128,512]{1,0:T(8,128)(2,1)S(1)} %get-tuple-element.3, bf16[512,512]{1,0:T(8,128)(2,1)S(1)} %copy-done.4, f32[192,512]{1,0:T(8,128)} %fusion.1), kind=kOutput, calls=%fused_computation.15 | convolution fusion | flops 67305472 | bytes 1310720 | tf_op jit(solution)/shard_map/dot_general | solution.py:94
  134.6 40.7 %all-gather.3.cloned.1.call-done = f32[20,64,512]{2,1,0:T(8,128)} async-done(((f32[5,64,512]{2,1,0:T(8,128)}), f32[20,64,512]{2,1,0:T(8,128)}) %all-gather.3.cloned.1.call-update) | async-done | bytes 2621456 | tf_op jit(solution)/shard_map/all_gather | solution.py:87
  175.3 2.9 %reduce_sum.9 = f32[5,64,512]{2,1,0:T(8,128)} reduce(f32[4,5,64,512]{3,2,1,0:T(8,128)} %bitcast.60, f32[]{:T(128)} %constant.6.clone.1), dimensions={0}, to_apply=%region_2.3 | reduce | flops 491520 | bytes 3276804 | tf_op jit(solution)/shard_map/reduce_sum | solution.py:87
  (27 shorter events, 3.4 us)
Async XLA Ops:
  7.2 24.0 %copy-start = (bf16[4,512,512]{2,1,0:T(8,128)(2,1)S(1)}, bf16[4,512,512]{2,1,0:T(8,128)(2,1)}, u32[]{:S(2)}) copy-start(bf16[4,512,512]{2,1,0:T(8,128)(2,1)} %param.11) | copy-start | bytes 6291460
  7.2 22.8 %copy-start.1 = (bf16[1,128,512]{2,1,0:T(8,128)(2,1)S(1)}, bf16[1,128,512]{2,1,0:T(8,128)(2,1)}, u32[]{:S(2)}) copy-start(bf16[1,128,512]{2,1,0:T(8,128)(2,1)} %param.9) | copy-start | bytes 393220
  11.1 18.8 %all-to-all-start = ((bf16[4,16,512]{2,1,0:T(8,128)(2,1)}), bf16[4,16,512]{2,1,0:T(8,128)(2,1)}, u32[]{:S(2)}, u32[]{:S(2)}) async-start(bf16[4,16,512]{2,1,0:T(8,128)(2,1)} %broadcast_select_fusion.1), calls=%async_computation | async-start | bytes 131072 | tf_op jit(solution)/shard_map/all_to_all | solution.py:12
  31.1 12.8 %copy-start.5 = (s32[1,64]{1,0:T(1,128)S(1)}, s32[1,64]{1,0:T(1,128)}, u32[]{:S(2)}) copy-start(s32[1,64]{1,0:T(1,128)} %param.16) | copy-start | bytes 772
  31.7 0.7 copy-start.3
  33.1 10.8 %all-to-all-start.1 = ((bf16[4,16,512]{2,1,0:T(8,128)(2,1)}), bf16[4,16,512]{2,1,0:T(8,128)(2,1)S(1)}, u32[]{:S(2)}, u32[]{:S(2)}) async-start(bf16[4,16,512]{2,1,0:T(8,128)(2,1)} %bitcast.10), calls=%async_computation.1 | async-start | bytes 131072 | tf_op jit(solution)/shard_map/all_to_all | solution.py:21
  49.2 9.7 %all-to-all-start.2 = ((bf16[4,16,512]{2,1,0:T(8,128)(2,1)}), bf16[4,16,512]{2,1,0:T(8,128)(2,1)}, u32[]{:S(2)}, u32[]{:S(2)}) async-start(bf16[4,16,512]{2,1,0:T(8,128)(2,1)} %broadcast_select_fusion), calls=%async_computation.2 | async-start | bytes 131072 | tf_op jit(solution)/shard_map/all_to_all | solution.py:12
  53.1 65.5 %reduce-scatter.2.cloned.1.call-start = ((), (), s32[]{:S(2)}) async-start(), calls=%async_computation.5 | async-start | bytes 5898240 | tf_op jit(solution)/shard_map/reduce_scatter | solution.py:86
  58.9 1.7 copy-start.2
  63.5 111.9 %all-gather.3.cloned.1.call-start = ((), (), s32[]{:S(2)}) async-start(), calls=%async_computation.6 | async-start | bytes 3276800 | tf_op jit(solution)/shard_map/all_gather | solution.py:87
  118.7 14.0 %copy-start.4 = (bf16[512,512]{1,0:T(8,128)(2,1)S(1)}, bf16[512,512]{1,0:T(8,128)(2,1)}, u32[]{:S(2)}) copy-start(bf16[512,512]{1,0:T(8,128)(2,1)} %param.12) | copy-start | bytes 1572868
Sparse Core Ops, SparseCore 0:
  63.6 54.9 reduce-scatter.1
  120.2 55.0 all-gather.2
